TPU v7x, 32 devices: a whole 2x2x4 slice. The times are simulated.
32 devices in a mesh: seq: 4 (over y, core), et: 8 (over z, x).
Axes of the slice: x: 2, y: 2, z: 4, core: 2. Of those that a mesh axis runs over, the one named last changes fastest.
Arguments:
- hidden_in: bfloat16 [128, 4096], P('seq'), may hold values from -6 to 6
- expert_ids: int32 [128, 2], P('seq'), may hold values from 0 to 7, all different within a row; in each aligned block of 32 rows (0 to 31, 32 to 63, ...) at most 10 rows name the same one
- gate_vals: bfloat16 [128, 2], P('seq'), may hold values from 0 to 1, as said below
- w_gate: bfloat16 [8, 4096, 14336], P('et', None, 'seq'), may hold values from -0.09375 to 0.09375
- w_up: bfloat16 [8, 4096, 14336], P('et', None, 'seq'), may hold values from -0.09375 to 0.09375
- w_down: bfloat16 [8, 14336, 4096], P('et', 'seq'), may hold values from -0.0625 to 0.0625
Outputs:
- mixed: bfloat16 [128, 4096], P('seq', 'et')
Inputs may be any that keep to these rules, and one draw needn't show every extreme that they name: `expert_ids`: the rows of each token name different experts; within each block of 32 rows (the rows of one device) no expert is named by more than 10 rows. `gate_vals`: each token's two weights sum to 1 up to bfloat16 rounding, the first is not the smaller.
All inputs are finite; a program needn't handle non-finite values.
Results may differ from a plain program's by a relative error of at most 0.019.
Values may be sent and summed in bfloat16 or wider, within the bound.
A program may use at most 128 MiB of HBM per device.

v0:
```python
import jax
import jax.numpy as jnp
from jax import lax
from jax.sharding import PartitionSpec as P

EXPERTS = 8
SLOTS = 10


def slot_numbers(routed):
    flattened = routed.reshape(-1)
    one_hot = (flattened[:, None] == jnp.arange(EXPERTS, dtype=jnp.int32)[None, :]).astype(
        jnp.int32
    )
    earlier = jnp.cumsum(one_hot, axis=0) - one_hot
    return jnp.sum(earlier * one_hot, axis=1).reshape(routed.shape)


def local(hidden_in, expert_ids, gate_vals, w_gate, w_up, w_down):
    group_size = lax.axis_size("et") // EXPERTS
    expert_here = lax.axis_index("et") // group_size
    slot_index = slot_numbers(expert_ids)
    chosen = expert_ids == expert_here
    columns = jnp.arange(SLOTS, dtype=jnp.int32)
    matches = chosen[:, None, :] & (slot_index[:, None, :] == columns[None, :, None])
    placing = jnp.any(matches, axis=2).astype(jnp.bfloat16)
    combining = jnp.sum(jnp.where(matches, gate_vals.astype(jnp.float32)[:, None, :], 0.0), axis=2)
    buffer = jnp.dot(placing.T, hidden_in, preferred_element_type=jnp.float32).astype(jnp.bfloat16)
    gate_local = w_gate[0]
    up_local = w_up[0]
    down_local = w_down[0]
    segment = lax.all_gather(buffer, "seq", axis=0, tiled=True)
    gate_part = jnp.dot(segment, gate_local, preferred_element_type=jnp.float32)
    up_part = jnp.dot(segment, up_local, preferred_element_type=jnp.float32)
    activations = (jax.nn.silu(gate_part) * up_part).astype(jnp.bfloat16)
    partial_value = lax.psum_scatter(
        jnp.dot(activations, down_local, preferred_element_type=jnp.float32).astype(jnp.bfloat16),
        "seq",
        scatter_dimension=0,
        tiled=True,
    ).astype(jnp.float32)
    contribution = jnp.dot(combining, partial_value, precision=lax.Precision.HIGHEST)
    share_width = hidden_in.shape[1] // lax.axis_size("et")
    mixed_part = lax.psum_scatter(
        contribution.astype(jnp.bfloat16), "et", scatter_dimension=1, tiled=True
    ).astype(jnp.float32)
    residual_part = lax.dynamic_slice_in_dim(
        hidden_in, lax.axis_index("et") * share_width, share_width, 1
    )
    return (residual_part.astype(jnp.float32) + mixed_part).astype(jnp.bfloat16)


def solution(mesh):
    in_specs = (
        P("seq", None),
        P("seq", None),
        P("seq", None),
        P("et", None, "seq"),
        P("et", None, "seq"),
        P("et", "seq", None),
    )
    out_specs = P("seq", "et")
    return jax.shard_map(local, mesh=mesh, in_specs=in_specs, out_specs=out_specs, check_vma=False)
```

profile of v0, /device:TPU:0, one launch (start us, length us, event | category | flops | bytes accessed | tf_op | source)
XLA Modules:
  0.0 160.5 jit_solution(4706864495786998253)
XLA Ops:
  6.5 0.0 all-reduce.3.cloned.1.call-start
  6.5 0.8 copy.16
  7.3 0.1 eq.38
  7.4 0.1 fusion.27
  7.5 0.1 reduce_window_sum.11
  7.6 0.2 select_reduce_fusion
  7.8 0.1 eq.42
  7.9 0.1 copy.17
  8.0 0.7 broadcast_compare_fusion
  8.7 1.1 fusion.19
  9.8 8.7 %all-gather = bf16[4,10,4096]{2,1,0:T(8,128)(2,1)S(1)} all-gather(bf16[1,10,4096]{2,1,0:T(8,128)(2,1)S(1)} %fusion.19), channel_id=1, replica_groups=mesh['seq'=4,'et'=8] {'seq'}, dimensions={0}, use_global_device_ids=true | all-gather | bytes 409600 | tf_op jit(solution)/shard_map/all_gather | solution.py:32
  18.5 0.1 reshape.5
  18.6 11.9 %fusion.4 = f32[40,3584]{1,0:T(8,128)S(1)} fusion(bf16[40,4096]{1,0:T(8,128)(2,1)S(1)} %reshape.5, bf16[1,4096,3584]{2,1,0:T(8,128)(2,1)} %param.9), kind=kOutput, calls=%fused_computation.4 | convolution fusion | flops 1174405120 | bytes 30261248 | tf_op jit(solution)/shard_map/dot_general | solution.py:33
  30.5 0.0 copy-start
  30.5 0.0 copy-start.1
  30.5 22.5 %fusion.14 = bf16[40,4096]{1,0:T(8,128)(2,1)} fusion(bf16[1,3584,4096]{2,1,0:T(8,128)(2,1)} %param.11, bf16[40,4096]{1,0:T(8,128)(2,1)S(1)} %reshape.5, bf16[1,4096,3584]{2,1,0:T(8,128)(2,1)} %param.10, f32[40,3584]{1,0:T(8,128)S(1)} %fusion.4), kind=kOutput, calls=%fused_computation.8 | convolution fusion | flops 2349834240 | bytes 59949056 | tf_op jit(solution)/shard_map/dot_general | solution.py:37
  53.0 0.0 all-reduce.3.cloned.1.call-update
  53.0 0.0 reduce-scatter.2.cloned.1.call-start
  53.1 0.6 dynamic-slice
  54.3 32.2 %all-reduce.3.cloned.1.call-done = bf16[40,4096]{1,0:T(8,128)(2,1)} async-done(((bf16[40,4096]{1,0:T(8,128)(2,1)}), bf16[40,4096]{1,0:T(8,128)(2,1)}) %all-reduce.3.cloned.1.call-update) | async-done | bytes 327696
  86.5 2.0 %convolution_convert_fusion = bf16[32,4096]{1,0:T(8,128)(2,1)} fusion(f32[32,10]{0,1:T(8,128)S(1)} %select_reduce_fusion.1, bf16[40,4096]{1,0:T(8,128)(2,1)} %all-reduce.3.cloned.1.call-done, u32[]{:T(128)S(6)} %multiply.1), kind=kOutput, calls=%fused_computation.9 | convolution fusion | flops 15859712 | bytes 394500 | tf_op jit(solution)/shard_map/dot_general | solution.py:42
  88.6 0.0 reduce-scatter.2.cloned.1.call-update
  88.6 63.7 %reduce-scatter.2.cloned.1.call-done = bf16[32,512]{1,0:T(8,128)(2,1)} async-done(((bf16[32,4096]{1,0:T(8,128)(2,1)}), bf16[32,512]{1,0:T(8,128)(2,1)}) %reduce-scatter.2.cloned.1.call-update) | async-done | bytes 32784 | tf_op jit(solution)/shard_map/reduce_scatter | solution.py:44
  152.3 1.4 add_convert_fusion
  (5 shorter events, 0.0 us)
Async XLA Ops:
  6.5 80.0 %all-reduce.3.cloned.1.call-start = ((), (), s32[]{:S(2)}) async-start(), calls=%async_computation.2 | async-start | bytes 655360
  30.5 22.6 %copy-start = (bf16[32,2]{0,1:T(2,128)(2,1)S(1)}, bf16[32,2]{0,1:T(2,128)(2,1)}, u32[]{:S(2)}) copy-start(bf16[32,2]{0,1:T(2,128)(2,1)} %param.8) | copy-start | bytes 388
  30.5 22.6 %copy-start.1 = (u32[32]{0:T(128)S(1)}, u32[32]{0:T(128)}, u32[]{:S(2)}) copy-start(u32[32]{0:T(128)} %constant.37) | copy-start | bytes 388
  53.0 99.3 %reduce-scatter.2.cloned.1.call-start = ((), (), s32[]{:S(2)}) async-start(), calls=%async_computation.1 | async-start | bytes 294912 | tf_op jit(solution)/shard_map/reduce_scatter | solution.py:44
Sparse Core Ops, SparseCore 0:
  53.1 33.3 all-reduce.2
  89.9 62.3 reduce-scatter.1
where the time goes:
time: 161 us
  waiting for transfers between devices  95.9 us (60%)
  matrix products  37.5 us (23%)
  between operations  14.2 us (9%)
  blocking collectives  8.68 us (5%)
  other arithmetic  2.48 us (2%)
  local copies, waits for them, and re-layouts  1.76 us (1%)
    reduce_scatter x1, waiting for transfers between devices, local(): lax.psum_scatter(contribution.astype(jnp.bfloat16), 'et', scatter_dimensi...  63.7 us
    unnamed x3, waiting for transfers between devices  32.2 us
    dot_general x1, matrix products, local(): jnp.dot(activations, down_local, preferred_element_type=jnp.float32)  22.5 us
    dot_general x1, matrix products, local(): gate_part = jnp.dot(segment, gate_local, preferred_element_type=jnp.float32)  11.9 us
    all_gather x1, blocking collectives, local(): segment = lax.all_gather(buffer, 'seq', axis=0, tiled=True)  8.68 us
  transfers between devices with their start and end apart: 2, of which 2 were waited for; matrix products, arithmetic and copies ran while one was open for 0% of the time, Pallas kernels for 0%

commit v1 on v0

--- a/solution.py
+++ b/solution.py
@@ -1,10 +1,19 @@
+import functools
+
 import jax
 import jax.numpy as jnp
 from jax import lax
+from jax.experimental import pallas as pl
+from jax.experimental.pallas import tpu as pltpu
 from jax.sharding import PartitionSpec as P
 
 EXPERTS = 8
 SLOTS = 10
+PAD = 16
+WIDE = 512
+DEPTH = 3
+LAG = 3
+MESH = pl.DeviceIdType.MESH
 
 
 def slot_numbers(routed):
@@ -50,6 +59,224 @@
     return (residual_part.astype(jnp.float32) + mixed_part).astype(jnp.bfloat16)
 
 
+def kernel(
+    n_et, n_wide,
+    hidden, ids, gates, w_gate, w_up, w_down, out,
+    xg, gu, dw, act, psend, precv, esend, erecv,
+    gu_sem, d_sem, x_send, x_recv, p_send, p_recv, e_send, e_recv,
+):
+    seq, et = lax.axis_index("seq"), lax.axis_index("et")
+    chip, core = seq // 2, seq % 2
+    mate = chip * 2 + (1 - core)
+    across = (1 - chip) * 2 + core
+    corner = (1 - chip) * 2 + (1 - core)
+    peers = (mate, across, corner)
+    share = out.shape[1]
+    half = hidden.shape[1] // 2
+    tokens = hidden.shape[0]
+    rows = 4 * PAD
+
+    def pair(i):
+        slot = i % DEPTH
+        cols = pl.ds(pl.multiple_of(i * WIDE, WIDE), WIDE)
+        return [
+            pltpu.make_async_copy(w.at[0, :, cols], gu.at[k, slot], gu_sem.at[k, slot])
+            for k, w in enumerate((w_gate, w_up))
+        ]
+
+    def target(i):
+        return (et + 1 + i) % n_et
+
+    def down(i):
+        cols = pl.ds(pl.multiple_of(target(i) * share, share), share)
+        return pltpu.make_async_copy(w_down.at[0, :, cols], dw.at[i], d_sem.at[i])
+
+    def start_pair(i):
+        for copy in pair(i):
+            copy.start()
+
+    for i in range(DEPTH):
+        start_pair(i)
+    down(0).start()
+    down(1).start()
+
+    barrier = pltpu.get_barrier_semaphore()
+    for p in peers:
+        pl.semaphore_signal(barrier, inc=1, device_id=(p, et), device_id_type=MESH)
+    for i in range(n_et - 1):
+        pl.semaphore_signal(barrier, inc=1, device_id=(seq, target(i)), device_id_type=MESH)
+
+    first, second = ids[:, 0:1], ids[:, 1:2]
+    earlier = (
+        lax.broadcasted_iota(jnp.int32, (tokens, tokens), 1)
+        < lax.broadcasted_iota(jnp.int32, (tokens, tokens), 0)
+    ).astype(jnp.float32).astype(jnp.bfloat16)
+    column = lax.broadcasted_iota(jnp.int32, (tokens, n_et * PAD), 1)
+
+    def matched(expert, slot):
+        named = ((first == expert) | (second == expert)).astype(jnp.float32)
+        before = jnp.dot(earlier, named.astype(jnp.bfloat16), preferred_element_type=jnp.float32)
+        return jnp.where(before == slot.astype(jnp.float32), named, 0.0)
+
+    here = matched(jnp.full_like(column, 0) + et, column)
+    placing = jnp.transpose(here)[:PAD, :].astype(jnp.bfloat16)
+    xg[seq] = jnp.dot(placing, hidden[...], preferred_element_type=jnp.float32).astype(jnp.bfloat16)
+
+    pl.semaphore_wait(barrier, len(peers) + n_et - 1)
+
+    def move(block, cols, to, n):
+        return pltpu.make_async_remote_copy(
+            src_ref=xg.at[block, :, cols], dst_ref=xg.at[block, :, cols],
+            send_sem=x_send.at[n], recv_sem=x_recv.at[n],
+            device_id=(to, et), device_id_type=MESH,
+        )
+
+    halves = (pl.ds(0, half), pl.ds(half, half))
+    far = [move(seq, halves[h], across, h) for h in range(2)]
+    near = [move(seq, halves[h], mate, 2 + h) for h in range(2)]
+    for copy in far + near:
+        copy.start()
+    relay = [move(across, halves[h], mate, 4 + h) for h in range(2)]
+    for h in range(2):
+        far[h].wait_recv()
+        relay[h].start()
+    for copy in near + relay:
+        copy.wait_recv()
+
+    def up_step(i, carry):
+        slot = i % DEPTH
+        for copy in pair(i):
+            copy.wait()
+        x = xg[...].reshape(rows, 2 * half)
+        g = jnp.dot(x, gu[0, slot], preferred_element_type=jnp.float32)
+        u = jnp.dot(x, gu[1, slot], preferred_element_type=jnp.float32)
+        act[:, pl.ds(pl.multiple_of(i * WIDE, WIDE), WIDE)] = (
+            g / (1.0 + jnp.exp(-g)) * u
+        ).astype(jnp.bfloat16)
+
+        @pl.when(i + DEPTH < n_wide)
+        def _():
+            start_pair(i + DEPTH)
+
+        @pl.when((i >= 2) & (i < n_et))
+        def _():
+            down(i).start()
+
+        return carry
+
+    lax.fori_loop(0, n_wide, up_step, 0)
+    for i in range(max(2, min(n_wide, n_et)), n_et):
+        down(i).start()
+
+    def scatter(i):
+        return [
+            pltpu.make_async_remote_copy(
+                src_ref=psend.at[i, p], dst_ref=precv.at[i, r],
+                send_sem=p_send.at[i, r], recv_sem=p_recv.at[i, r],
+                device_id=(p, et), device_id_type=MESH,
+            )
+            for r, p in enumerate(peers)
+        ]
+
+    def give(i):
+        return pltpu.make_async_remote_copy(
+            src_ref=esend.at[i], dst_ref=erecv.at[i],
+            send_sem=e_send.at[i], recv_sem=e_recv.at[i],
+            device_id=(seq, target(i)), device_id_type=MESH,
+        )
+
+    def summed(i):
+        for copy in scatter(i):
+            copy.wait_recv()
+        total = psend[i, seq].astype(jnp.float32)
+        for r in range(len(peers)):
+            total = total + precv[i, r].astype(jnp.float32)
+        return total.astype(jnp.bfloat16)
+
+    def pass_on(i):
+        esend[i] = summed(i)
+        give(i).start()
+
+    def down_step(i, carry):
+        down(i).wait()
+        part = jnp.dot(act[...], dw[i], preferred_element_type=jnp.float32)
+        psend[i] = part.astype(jnp.bfloat16).reshape(4, PAD, share)
+        for copy in scatter(i):
+            copy.start()
+
+        @pl.when(i >= LAG)
+        def _():
+            pass_on(i - LAG)
+
+        return carry
+
+    lax.fori_loop(0, n_et, down_step, 0)
+    for i in range(n_et - LAG, n_et - 1):
+        pass_on(i)
+
+    source = et + n_et - 1 - column // PAD
+    source = jnp.where(source >= n_et, source - n_et, source)
+    weight = jnp.where(
+        first == source, gates[:, 0:1].astype(jnp.float32), gates[:, 1:2].astype(jnp.float32)
+    )
+    combining = (matched(source, column % PAD) * weight).astype(jnp.bfloat16)
+    residual = hidden[:, pl.ds(pl.multiple_of(et * share, share), share)].astype(jnp.float32)
+
+    erecv[n_et - 1] = summed(n_et - 1)
+    for i in range(n_et - 1):
+        give(i).wait_recv()
+    mixed = jnp.dot(
+        combining, erecv[...].reshape(n_et * PAD, share), preferred_element_type=jnp.float32
+    )
+    out[...] = (residual + mixed).astype(jnp.bfloat16)
+
+    for copy in far + near + relay:
+        copy.wait_send()
+    for i in range(n_et):
+        for copy in scatter(i):
+            copy.wait_send()
+    for i in range(n_et - 1):
+        give(i).wait_send()
+
+
+def fused(hidden_in, expert_ids, gate_vals, w_gate, w_up, w_down):
+    n_et = lax.axis_size("et")
+    tokens, width = hidden_in.shape
+    units = w_gate.shape[2]
+    share = width // n_et
+    n_wide = units // WIDE
+    vmem = pl.BlockSpec(memory_space=pltpu.VMEM)
+    hbm = pl.BlockSpec(memory_space=pl.ANY)
+    dma = pltpu.SemaphoreType.DMA
+    return pl.pallas_call(
+        functools.partial(kernel, n_et, n_wide),
+        out_shape=jax.ShapeDtypeStruct((tokens, share), jnp.bfloat16),
+        in_specs=[vmem] * 3 + [hbm] * 3,
+        out_specs=vmem,
+        scratch_shapes=[
+            pltpu.VMEM((4, PAD, width), jnp.bfloat16),
+            pltpu.VMEM((2, DEPTH, width, WIDE), jnp.bfloat16),
+            pltpu.VMEM((n_et, units, share), jnp.bfloat16),
+            pltpu.VMEM((4 * PAD, units), jnp.bfloat16),
+            pltpu.VMEM((n_et, 4, PAD, share), jnp.bfloat16),
+            pltpu.VMEM((n_et, 3, PAD, share), jnp.bfloat16),
+            pltpu.VMEM((n_et, PAD, share), jnp.bfloat16),
+            pltpu.VMEM((n_et, PAD, share), jnp.bfloat16),
+            dma((2, DEPTH)),
+            dma((n_et,)),
+            dma((6,)),
+            dma((6,)),
+            dma((n_et, 3)),
+            dma((n_et, 3)),
+            dma((n_et,)),
+            dma((n_et,)),
+        ],
+        compiler_params=pltpu.CompilerParams(
+            collective_id=0, has_side_effects=True, vmem_limit_bytes=66_000_000
+        ),
+    )(hidden_in, expert_ids, gate_vals, w_gate, w_up, w_down)
+
+
 def solution(mesh):
     in_specs = (
         P("seq", None),
@@ -60,4 +287,16 @@
         P("et", "seq", None),
     )
     out_specs = P("seq", "et")
-    return jax.shard_map(local, mesh=mesh, in_specs=in_specs, out_specs=out_specs, check_vma=False)
+    n_seq, n_et = mesh.shape["seq"], mesh.shape["et"]
+
+    def layer(hidden_in, expert_ids, gate_vals, w_gate, w_up, w_down):
+        width, units = w_gate.shape[1:]
+        held = 2 * (2 * DEPTH * width * WIDE + units * width)
+        fits = (
+            n_seq == 4 and n_et == EXPERTS and units % WIDE == 0
+            and units // WIDE > DEPTH and width % (n_et * 128) == 0 and held < 58_000_000
+        )
+        body = fused if fits else local
+        return body(hidden_in, expert_ids, gate_vals, w_gate, w_up, w_down)
+
+    return jax.shard_map(layer, mesh=mesh, in_specs=in_specs, out_specs=out_specs, check_vma=False)

time: 161 us -> 44.5 us (0.28)
  waiting for transfers between devices: 95.9 us -> 0 us
  Pallas kernels: 0 us -> 40.2 us
  matrix products: 37.5 us -> 0 us
  between operations: 14.2 us -> 0.01 us
  blocking collectives: 8.68 us -> 0 us
  other arithmetic: 2.48 us -> 0 us
  local copies, waits for them, and re-layouts: 1.76 us -> 4.07 us
    reduce_scatter x1 -> x0, waiting for transfers between devices: 63.7 us -> none  [local(): lax.psum_scatter(contribution.astype(jnp.bfloat16), 'et', scatter_dimensi...]
    pallas_call x0 -> x1, Pallas kernels: none -> 40.2 us  [fused(): pl.pallas_call(functools.partial(kernel, n_et, n_wide), out_shape=jax.Sha...]
    dot_general x4 -> x0, matrix products: 37.5 us -> none  [the longest x1 22.5 us: local(): jnp.dot(activations, down_local, preferred_element_type=jnp.float32)]
    unnamed x3 -> x0, waiting for transfers between devices: 32.2 us -> none
    all_gather x1 -> x0, blocking collectives: 8.68 us -> none  [local(): segment = lax.all_gather(buffer, 'seq', axis=0, tiled=True)]
    unnamed x7 -> x3, local copies, waits for them, and re-layouts: 1.48 us -> 4.07 us
  transfers between devices with their start and end apart: 2 -> 0, of which waited for: 2 -> 0; matrix products, arithmetic and copies ran while one was open for 0% -> 0% of each run, Pallas kernels for 0% -> 0%
where the time goes in v1:
time: 44.5 us; the launch traced here: 44.3 us
  Pallas kernels  40.2 us (90%)
  local copies, waits for them, and re-layouts  4.07 us (9%)
    pallas_call x1, Pallas kernels, fused(): pl.pallas_call(functools.partial(kernel, n_et, n_wide), out_shape=jax.Sha...  40.2 us
    unnamed x3, local copies, waits for them, and re-layouts  4.07 us

profile of v1, /device:TPU:0, one launch (start us, length us, event | category | flops | bytes accessed | tf_op | source)
XLA Modules:
  0.0 44.3 jit_solution(16415031354135776836)
XLA Ops:
  0.0 1.3 %copy.8.gates = bf16[32,2]{1,0:T(8,128)(2,1)} copy(bf16[32,2]{0,1:T(2,128)(2,1)} %param.8) | data formatting | bytes 256 | tf_op args[2]
  1.3 1.4 %copy.7.ids = s32[32,2]{1,0:T(8,128)} copy(s32[32,2]{0,1:T(2,128)} %param.7) | data formatting | bytes 512 | tf_op args[1]
  2.7 40.2 %shard_map.64 = bf16[32,512]{1,0:T(8,128)(2,1)} custom-call(bf16[32,4096]{1,0:T(8,128)(2,1)} %hidden.1, s32[32,2]{1,0:T(8,128)} %copy.7.ids, bf16[32,2]{1,0:T(8,128)(2,1)} %copy.8.gates, bf16[1,4096,3584]{2,1,0:T(8,128)(2,1)} %w_gate.1, bf16[1,4096,3584]{2,1,0:T(8,128)(2,1)} %w_up.1, bf16[1,3584,4096]{2,1,0:T(8,128)(2,1)} %w_down.1), custom_call_target="tpu_custom_call" | custom-call | tf_op jit(solution)/shard_map/pallas_call | solution.py:251
  42.9 1.4 %copy.10 = bf16[32,512]{1,0:T(8,128)(2,1)} copy(bf16[32,512]{1,0:T(8,128)(2,1)} %shard_map.64) | data formatting | bytes 65536
